TPU v7x, 32 devices: a whole 2x2x4 slice. The times are simulated.
32 devices in a mesh: mesh: 8 (over y, x, core), harm: 4 (over z).
Axes of the slice: x: 2, y: 2, z: 4, core: 2. Of those that a mesh axis runs over, the one named last changes fastest.
Arguments:
- field_in: float32 [64, 40960], P('harm', 'mesh'), may hold values from -6 to 6
- faces: int32 [2, 8192], P(None, 'mesh'), may hold values from 0 to 5119, as said below
- connectivity: int32 [6, 32768], P(None, 'mesh'), may hold values from 0 to 7167
- curl_vectors: float32 [3, 6, 32768], P(None, None, 'mesh'), may hold values from -2.4 to 2.4
- operating_point: float32 [64, 3, 8, 4096], P(None, None, None, ('mesh', 'harm')), may hold values from -2.5 to 2.5
- material: int32 [8, 4096], P(None, ('mesh', 'harm')), may hold values from 0 to 3
- bh_knots: int32 [8], replicated, may hold values from 0 to 15
- curve_base: float32 [4], replicated, may hold values from 0.5 to 2
- curve_slopes: float32 [4, 8], replicated, may hold values from 0.02 to 0.2
Outputs:
- product: float32 [64, 40960], P('harm', 'mesh')
Inputs may be any that keep to these rules, and one draw needn't show every extreme that they name: `faces`: for each partition the 1024 lower face edges and the 1024 upper face edges are 2048 distinct local edge numbers. `connectivity`: numbers below 5120 are the partition's own edges, the next 1024 the ghost edges after the upper face list of the partition below, the last 1024 those after the lower face list of the partition above.
All inputs are finite; a program needn't handle non-finite values.
Results may differ from a plain program's by a relative error of at most 0.0003.
Values sent between devices are 32-bit elements; how exact they have to be, the bound alone decides.
No kernel may reach another device: no remote copies, remote signals or barrier semaphores. Data moves between devices by JAX's collectives and lax.ppermute only.
A program may use at most 128 MiB of HBM per device.

v0:
```python
import jax
import jax.numpy as jnp
from jax import lax
from jax.sharding import PartitionSpec as P

KNOT_STEP = 0.25
KNOT_WIDTH = 0.5


def with_halo(value, sides, width):
    for axis, dim in sides:
        count, length = (lax.axis_size(axis), value.shape[dim])
        up = [(i, (i + 1) % count) for i in range(count)]
        down = [(j, i) for i, j in up]
        last = lax.slice_in_dim(value, length - width, length, axis=dim)
        first = lax.slice_in_dim(value, 0, width, axis=dim)
        before = lax.ppermute(last, axis, up)
        after = lax.ppermute(first, axis, down)
        value = jnp.concatenate([before, value, after], axis=dim)
    return value


def dft_tables(length):
    sample_idx = jnp.arange(length, dtype=jnp.int32)
    coef_idx = jnp.arange(length, dtype=jnp.int32)
    half_len = length // 2
    harmonic = jnp.where(coef_idx < half_len, coef_idx, coef_idx - half_len + 1)
    harmonic = jnp.where(coef_idx == length - 1, half_len, harmonic)
    is_sine = (coef_idx >= half_len) & (coef_idx < length - 1)
    phase_int = harmonic[:, None] * sample_idx[None, :] % length
    angles = phase_int.astype(jnp.float32) * (2.0 * jnp.pi / length)
    basis_rows = jnp.where(is_sine[:, None], jnp.sin(angles), jnp.cos(angles))
    weight = jnp.where((coef_idx == 0) | (coef_idx == length - 1), 1.0 / length, 2.0 / length)
    return (basis_rows.T, basis_rows * weight[:, None].astype(jnp.float32))


def apply_tensor(flux_step, point, material, bh_knots, curve_base, curve_slopes):
    kind_ids = jnp.arange(curve_base.shape[0], dtype=jnp.int32).reshape(
        (-1,) + (1,) * material.ndim
    )
    one_hot = (material[None] == kind_ids).astype(jnp.float32)
    base_elem = jnp.einsum("a,a...->...", curve_base, one_hot, precision=lax.Precision.HIGHEST)
    slope_elem = jnp.einsum("ak,a...->k...", curve_slopes, one_hot, precision=lax.Precision.HIGHEST)
    flux_sq = jnp.sum(point * point, axis=1)
    knot_pos = bh_knots.astype(jnp.float32) * KNOT_STEP
    scaled = (flux_sq[None] - knot_pos.reshape((-1,) + (1,) * flux_sq.ndim)) / KNOT_WIDTH
    reluct = base_elem[None] + jnp.sum(slope_elem[:, None] * jax.nn.softplus(scaled), axis=0)
    slope_sum = jnp.sum(slope_elem[:, None] * jax.nn.sigmoid(scaled), axis=0) / KNOT_WIDTH
    projected = jnp.sum(point * flux_step, axis=1)
    return reluct[:, None] * flux_step + 2.0 * (slope_sum * projected)[:, None] * point


def per_device(
    field_in,
    faces,
    connectivity,
    curl_vectors,
    operating_point,
    material,
    bh_knots,
    curve_base,
    curve_slopes,
):
    coeffs = field_in.shape[0]
    own_edges = field_in.shape[1]
    face_len = faces.shape[1]
    elements = connectivity.shape[1]
    mesh_count = lax.axis_size("mesh")
    harm_count = lax.axis_size("harm")
    block_len = operating_point.shape[3]
    samples = coeffs * harm_count
    lower_face = field_in[:, faces[0]]
    upper_face = field_in[:, faces[1]]
    padded = with_halo(jnp.concatenate([lower_face, upper_face], axis=1), (("mesh", 1),), face_len)
    extended = jnp.concatenate([field_in, padded[:, :face_len], padded[:, 3 * face_len :]], axis=1)
    gathered = extended[:, connectivity]
    curl_part = jnp.einsum("ije,cje->cie", curl_vectors, gathered, precision=lax.Precision.HIGHEST)
    arrived = lax.all_to_all(
        lax.all_to_all(
            curl_part.reshape(coeffs, 3, mesh_count, 1, harm_count, 1, block_len),
            "mesh",
            split_axis=2,
            concat_axis=3,
            tiled=True,
        ),
        "harm",
        split_axis=4,
        concat_axis=5,
        tiled=True,
    )
    arrived = arrived.reshape(coeffs, 3, mesh_count, harm_count, block_len)
    inverse, forward = dft_tables(samples)
    inverse_blocks = inverse.reshape(samples, harm_count, coeffs)
    flux_step = jnp.einsum(
        "thk,kimhe->time", inverse_blocks, arrived, precision=lax.Precision.HIGHEST
    )
    field_step = apply_tensor(
        flux_step, operating_point, material, bh_knots, curve_base, curve_slopes
    )
    forward_blocks = forward.reshape(harm_count, coeffs, samples)
    outgoing = jnp.einsum(
        "hkt,time->kimhe", forward_blocks, field_step, precision=lax.Precision.HIGHEST
    )
    returned = lax.all_to_all(
        lax.all_to_all(
            outgoing.reshape(coeffs, 3, 1, mesh_count, 1, harm_count, block_len),
            "mesh",
            split_axis=3,
            concat_axis=2,
            tiled=True,
        ),
        "harm",
        split_axis=5,
        concat_axis=4,
        tiled=True,
    )
    field_part = returned.reshape(coeffs, 3, elements)
    contrib = jnp.einsum("ije,cie->cje", curl_vectors, field_part, precision=lax.Precision.HIGHEST)
    assembled = (
        jnp.zeros((coeffs, own_edges + 2 * face_len), jnp.float32)
        .at[:, connectivity.reshape(-1)]
        .add(contrib.reshape(coeffs, -1))
    )
    ghost_sums = with_halo(assembled[:, own_edges:], (("mesh", 1),), face_len)
    result = assembled[:, :own_edges].at[:, faces[0]].add(ghost_sums[:, :face_len])
    result = result.at[:, faces[1]].add(ghost_sums[:, 3 * face_len :])
    return result


def solution(mesh):
    return jax.shard_map(
        per_device,
        mesh=mesh,
        in_specs=(
            P("harm", "mesh"),
            P(None, "mesh"),
            P(None, "mesh"),
            P(None, None, "mesh"),
            P(None, None, None, ("mesh", "harm")),
            P(None, ("mesh", "harm")),
            P(),
            P(),
            P(),
        ),
        out_specs=P("harm", "mesh"),
        check_vma=False,
    )
```

profile of v0, /device:TPU:1, one launch (start us, length us, event | category | flops | bytes accessed | tf_op | source)
XLA Modules:
  0.0 467.0 jit_solution(17183202074254305449)
XLA Ops:
  2.6 4.0 gather_fusion
  9.2 4.0 gather_fusion.1
  14.8 6.7 %copy.84 = f32[3,6,4096]{1,0,2:T(4,128)} copy(f32[3,6,4096]{2,1,0:T(8,128)} %param.12) | data formatting | bytes 589824 | tf_op args[3]
  22.9 3.1 pad_maximum_fusion
  26.0 83.9 %gather_fusion.2 = f32[24576,16]{1,0:T(8,128)} fusion(f32[16,7168]{0,1:T(8,128)} %pad_maximum_fusion, s32[24576]{0:T(1024)S(1)} %broadcast_clamp_fusion), kind=kCustom, calls=%fused_computation.2 | custom fusion | bytes 3244032 | tf_op jit(solution)/shard_map/gather | solution.py:76
  109.9 39.5 %fusion = f32[4096,16,3]{1,2,0:T(4,128)} fusion(f32[3,6,4096]{1,0,2:T(4,128)} %copy.84, f32[6,4096,16]{2,1,0:T(8,128)} %bitcast.78), kind=kOutput, calls=%fused_computation.6 | convolution fusion | flops 14155776 | bytes 2654208 | tf_op jit(solution)/shard_map/ije,cje->cie/dot_general | solution.py:77
  149.3 7.5 %copy.85 = f32[16,3,8,1,4,1,128]{6,0,4,1,5,3,2:T(8,128)} copy(f32[16,3,8,1,4,1,128]{0,1,6,4,2,5,3:T(4,128)} %bitcast.77) | data formatting | bytes 1572864 | tf_op jit(solution)/shard_map/reshape | solution.py:80
  156.8 3.6 all-to-all-start
  160.9 8.6 %all-to-all-done = f32[16,3,8,1,4,1,128]{6,0,4,1,5,3,2:T(8,128)S(1)} async-done(((f32[16,3,8,1,4,1,128]{6,0,4,1,5,3,2:T(8,128)}), f32[16,3,8,1,4,1,128]{6,0,4,1,5,3,2:T(8,128)S(1)}, u32[]{:S(2)}, u32[]{:S(2)}) %all-to-all-start) | async-done | bytes 786464 | tf_op jit(solution)/shard_map/all_to_all | solution.py:79
  170.5 4.8 %all-to-all-start.1 = ((f32[16,3,1,8,4,1,128]{6,0,3,1,5,2,4:T(8,128)}), f32[16,3,1,8,4,1,128]{6,0,3,1,5,2,4:T(8,128)S(1)}, u32[]{:S(2)}, u32[]{:S(2)}) async-start(f32[16,3,1,8,4,1,128]{6,0,3,1,5,2,4:T(8,128)} %copy.86), calls=%async_computation.1 | async-start | bytes 1572864 | tf_op jit(solution)/shard_map/all_to_all | solution.py:78
  177.5 16.0 %all-to-all-done.1 = f32[16,3,1,8,4,1,128]{6,0,3,1,5,2,4:T(8,128)S(1)} async-done(((f32[16,3,1,8,4,1,128]{6,0,3,1,5,2,4:T(8,128)}), f32[16,3,1,8,4,1,128]{6,0,3,1,5,2,4:T(8,128)S(1)}, u32[]{:S(2)}, u32[]{:S(2)}) %all-to-all-start.1) | async-done | bytes 786464 | tf_op jit(solution)/shard_map/all_to_all | solution.py:78
  197.2 7.7 %all-to-all-start.2 = ((f32[16,3,1,8,1,4,128]{6,0,5,1,4,2,3:T(8,128)}), f32[16,3,1,8,1,4,128]{6,0,5,1,4,2,3:T(8,128)S(1)}, u32[]{:S(2)}, u32[]{:S(2)}) async-start(f32[16,3,1,8,1,4,128]{6,0,5,1,4,2,3:T(8,128)} %copy.92), calls=%async_computation.2 | async-start | bytes 1572864 | tf_op jit(solution)/shard_map/all_to_all | solution.py:105
  205.0 9.0 %all-to-all-done.2 = f32[16,3,1,8,1,4,128]{6,0,5,1,4,2,3:T(8,128)S(1)} async-done(((f32[16,3,1,8,1,4,128]{6,0,5,1,4,2,3:T(8,128)}), f32[16,3,1,8,1,4,128]{6,0,5,1,4,2,3:T(8,128)S(1)}, u32[]{:S(2)}, u32[]{:S(2)}) %all-to-all-start.2) | async-done | bytes 786464 | tf_op jit(solution)/shard_map/all_to_all | solution.py:105
  215.0 3.5 all-to-all-start.3
  218.6 18.7 %all-to-all-done.3 = f32[16,3,8,1,1,4,128]{6,0,2,1,4,3,5:T(8,128)S(1)} async-done(((f32[16,3,8,1,1,4,128]{6,0,2,1,4,3,5:T(8,128)}), f32[16,3,8,1,1,4,128]{6,0,2,1,4,3,5:T(8,128)S(1)}, u32[]{:S(2)}, u32[]{:S(2)}) %all-to-all-start.3) | async-done | bytes 786464 | tf_op jit(solution)/shard_map/all_to_all | solution.py:104
  237.3 5.8 %copy.105 = f32[16,3,8,1,1,4,128]{0,1,6,5,2,4,3:T(4,128)} copy(f32[16,3,8,1,1,4,128]{6,0,2,1,4,3,5:T(8,128)S(1)} %all-to-all-done.3) | data formatting | bytes 1572864 | tf_op jit(solution)/shard_map/reshape | solution.py:117
  243.1 37.0 %convolution_bitcast_fusion = f32[16,6,4096]{0,1,2:T(8,128)} fusion(f32[16,3,4096]{0,1,2:T(4,128)} %bitcast.79, f32[3,6,4096]{1,0,2:T(4,128)} %copy.84), kind=kOutput, calls=%fused_computation.9 | convolution fusion | flops 14155776 | bytes 2654208 | tf_op jit(solution)/shard_map/ije,cie->cje/dot_general | solution.py:118
  280.2 9.6 %copy.97 = f32[16,6,4096]{2,1,0:T(8,128)S(1)} copy(f32[16,6,4096]{0,1,2:T(8,128)} %convolution_bitcast_fusion) | data formatting | bytes 3145728 | tf_op jit(solution)/shard_map/ije,cie->cje/transpose | solution.py:118
  291.9 7.6 %copy.98 = f32[24576,16]{1,0:T(8,128)} copy(f32[24576,16]{0,1:T(8,128)} %bitcast.81) | data formatting | bytes 3145728 | tf_op jit(solution)/shard_map/reshape | solution.py:122
  299.5 132.9 %scatter_custom_fusion = f32[16,7168]{0,1:T(8,128)} fusion(s32[24576]{0:T(1024)S(1)} %bitcast.86, f32[24576,16]{1,0:T(8,128)} %copy.98, f32[]{:T(128)} %constant.23.clone.1), kind=kCustom, calls=%fused_computation.16 | custom fusion | flops 393216 | bytes 459264 | tf_op jit(solution)/shard_map/scatter-add | solution.py:122
  433.9 5.3 %collective-permute-start.2 = (f32[16,1024]{0,1:T(8,128)S(1)}, f32[16,1024]{0,1:T(8,128)}, u32[]{:S(2)}, u32[]{:S(2)}) collective-permute-start(f32[16,1024]{0,1:T(8,128)S(1)} %get-tuple-element.8), channel_id=1, source_target_pairs={{0,4},{4,8},{8,12},{12,16},{16,20},{20,24},{24,28},{28,0},{1,5},{5... | collective-permute-start | bytes 196616 | tf_op jit(solution)/shard_map/ppermute | solution.py:17
  439.2 11.5 %collective-permute-done.2 = f32[16,1024]{0,1:T(8,128)} collective-permute-done((f32[16,1024]{0,1:T(8,128)S(1)}, f32[16,1024]{0,1:T(8,128)}, u32[]{:S(2)}, u32[]{:S(2)}) %collective-permute-start.2) | collective-permute-done | bytes 65568 | tf_op jit(solution)/shard_map/ppermute | solution.py:17
  450.7 7.4 %scatter_custom_fusion.1 = f32[16,5120]{0,1:T(8,128)S(1)} fusion(f32[16,5120]{0,1:T(8,128)S(1)} %slice-done, s32[1024]{0:T(1024)S(1)} %bitcast.90, f32[16,1024]{0,1:T(8,128)} %collective-permute-done.2), kind=kCustom, calls=%fused_computation.33 | custom fusion | flops 16384 | bytes 393216 | tf_op jit(solution)/shard_map/scatter-add | solution.py:125
  458.1 7.4 %scatter_custom_fusion.2 = f32[16,5120]{0,1:T(8,128)S(1)} fusion(f32[16,5120]{0,1:T(8,128)S(1)} %scatter_custom_fusion.1, s32[1024]{0:T(1024)S(1)} %bitcast.88, f32[16,1024]{0,1:T(8,128)} %collective-permute-done.3), kind=kCustom, calls=%fused_computation.31 | custom fusion | flops 16384 | bytes 393216 | tf_op jit(solution)/shard_map/scatter-add | solution.py:126
  (52 shorter events, 21.4 us)
Async XLA Ops:
  0.0 160.5 %copy-start = (f32[4,8]{1,0:T(4,128)S(1)}, f32[4,8]{1,0:T(4,128)}, u32[]{:S(2)}) copy-start(f32[4,8]{1,0:T(4,128)} %param.17) | copy-start | bytes 388
  0.0 13.2 %copy-start.3 = (s32[6,4096]{1,0:T(8,128)S(1)}, s32[6,4096]{1,0:T(8,128)}, u32[]{:S(2)}) copy-start(s32[6,4096]{1,0:T(8,128)} %param.11) | copy-start | bytes 294916
  6.6 15.0 %collective-permute-start = (f32[16,1024]{0,1:T(8,128)}, f32[16,1024]{0,1:T(8,128)S(1)}, u32[]{:S(2)}, u32[]{:S(2)}) collective-permute-start(f32[16,1024]{0,1:T(8,128)} %bitcast.91), channel_id=1, source_target_pairs={{0,4},{4,8},{8,12},{12,16},{16,20},{20,24},{24,28},{28,0},{1,5},{5... | collective-permute-start | bytes 196616 | tf_op jit(solution)/shard_map/ppermute | solution.py:17
  13.2 9.7 %collective-permute-start.1 = (f32[16,1024]{0,1:T(8,128)}, f32[16,1024]{0,1:T(8,128)}, u32[]{:S(2)}, u32[]{:S(2)}) collective-permute-start(f32[16,1024]{0,1:T(8,128)} %bitcast.92), channel_id=1, source_target_pairs={{4,0},{8,4},{12,8},{16,12},{20,16},{24,20},{28,24},{0,28},{5,1},{9... | collective-permute-start | bytes 196616 | tf_op jit(solution)/shard_map/ppermute | solution.py:18
  149.3 11.2 %copy-start.4 = (s32[8,128]{1,0:T(8,128)S(1)}, s32[8,128]{1,0:T(8,128)}, u32[]{:S(2)}) copy-start(s32[8,128]{1,0:T(8,128)} %param.14) | copy-start | bytes 12292
  149.3 11.4 %copy-start.5 = (s32[8]{0:T(128)S(1)}, s32[8]{0:T(128)}, u32[]{:S(2)}) copy-start(s32[8]{0:T(128)} %param.15) | copy-start | bytes 100
  149.3 11.4 %copy-start.6 = (f32[4]{0:T(128)S(1)}, f32[4]{0:T(128)}, u32[]{:S(2)}) copy-start(f32[4]{0:T(128)} %param.16) | copy-start | bytes 52
  156.8 18.4 %copy-start.2 = (f32[64,3,8,128]{3,2,1,0:T(8,128)S(1)}, f32[64,3,8,128]{3,2,1,0:T(8,128)}, u32[]{:S(2)}) copy-start(f32[64,3,8,128]{3,2,1,0:T(8,128)} %param.13) | copy-start | bytes 2359300
  156.8 12.6 %all-to-all-start = ((f32[16,3,8,1,4,1,128]{6,0,4,1,5,3,2:T(8,128)}), f32[16,3,8,1,4,1,128]{6,0,4,1,5,3,2:T(8,128)S(1)}, u32[]{:S(2)}, u32[]{:S(2)}) async-start(f32[16,3,8,1,4,1,128]{6,0,4,1,5,3,2:T(8,128)} %copy.85), calls=%async_computation | async-start | bytes 1572864 | tf_op jit(solution)/shard_map/all_to_all | solution.py:79
  170.5 23.0 %all-to-all-start.1 = ((f32[16,3,1,8,4,1,128]{6,0,3,1,5,2,4:T(8,128)}), f32[16,3,1,8,4,1,128]{6,0,3,1,5,2,4:T(8,128)S(1)}, u32[]{:S(2)}, u32[]{:S(2)}) async-start(f32[16,3,1,8,4,1,128]{6,0,3,1,5,2,4:T(8,128)} %copy.86), calls=%async_computation.1 | async-start | bytes 1572864 | tf_op jit(solution)/shard_map/all_to_all | solution.py:78
  197.2 16.9 %all-to-all-start.2 = ((f32[16,3,1,8,1,4,128]{6,0,5,1,4,2,3:T(8,128)}), f32[16,3,1,8,1,4,128]{6,0,5,1,4,2,3:T(8,128)S(1)}, u32[]{:S(2)}, u32[]{:S(2)}) async-start(f32[16,3,1,8,1,4,128]{6,0,5,1,4,2,3:T(8,128)} %copy.92), calls=%async_computation.2 | async-start | bytes 1572864 | tf_op jit(solution)/shard_map/all_to_all | solution.py:105
  215.0 22.3 %all-to-all-start.3 = ((f32[16,3,8,1,1,4,128]{6,0,2,1,4,3,5:T(8,128)}), f32[16,3,8,1,1,4,128]{6,0,2,1,4,3,5:T(8,128)S(1)}, u32[]{:S(2)}, u32[]{:S(2)}) async-start(f32[16,3,8,1,1,4,128]{6,0,2,1,4,3,5:T(8,128)} %copy.93), calls=%async_computation.3 | async-start | bytes 1572864 | tf_op jit(solution)/shard_map/all_to_all | solution.py:104
  432.4 18.2 %slice-start = ((f32[16,7168]{0,1:T(8,128)}), f32[16,5120]{0,1:T(8,128)S(1)}, s32[]{:S(2)}) async-start(f32[16,7168]{0,1:T(8,128)} %scatter_custom_fusion), calls=%async_computation.4 | async-start | bytes 5242880 | tf_op jit(solution)/shard_map/slice | solution.py:125
  433.9 16.8 %collective-permute-start.2 = (f32[16,1024]{0,1:T(8,128)S(1)}, f32[16,1024]{0,1:T(8,128)}, u32[]{:S(2)}, u32[]{:S(2)}) collective-permute-start(f32[16,1024]{0,1:T(8,128)S(1)} %get-tuple-element.8), channel_id=1, source_target_pairs={{0,4},{4,8},{8,12},{12,16},{16,20},{20,24},{24,28},{28,0},{1,5},{5... | collective-permute-start | bytes 196616 | tf_op jit(solution)/shard_map/ppermute | solution.py:17
  439.2 18.9 %collective-permute-start.3 = (f32[16,1024]{0,1:T(8,128)S(1)}, f32[16,1024]{0,1:T(8,128)}, u32[]{:S(2)}, u32[]{:S(2)}) collective-permute-start(f32[16,1024]{0,1:T(8,128)S(1)} %get-tuple-element.7), channel_id=1, source_target_pairs={{4,0},{8,4},{12,8},{16,12},{20,16},{24,20},{28,24},{0,28},{5,1},{9... | collective-permute-start | bytes 196616 | tf_op jit(solution)/shard_map/ppermute | solution.py:18
  450.7 16.3 %copy-start.1 = (f32[4,8]{1,0:T(4,128)S(1)}, f32[4,8]{1,0:T(4,128)}, u32[]{:S(2)}) copy-start(f32[4,8]{1,0:T(4,128)} %param.17) | copy-start | bytes 388
where the time goes:
time: 468 us; the launch traced here: 467 us
  other arithmetic  155 us (33%)
  local copies, waits for them, and re-layouts  140 us (30%)
  matrix products  79.3 us (17%)
  waiting for transfers between devices  65.2 us (14%)
  starting transfers between devices  27.6 us (6%)
    scatter-add x1, other arithmetic, per_device(): assembled = jnp.zeros((coeffs, own_edges + 2 * face_len), jnp.float32).at...  133 us
    gather x1, local copies, waits for them, and re-layouts, per_device(): gathered = extended[:, connectivity]  83.9 us
    dot_general x1, matrix products, per_device(): jnp.einsum('ije,cje->cie', curl_vectors, gathered, precision=lax.Precisio...  39.5 us
    dot_general x1, matrix products, per_device(): jnp.einsum('ije,cie->cje', curl_vectors, field_part, precision=lax.Precis...  37 us
    all_to_all x1, waiting for transfers between devices, per_device(): lax.all_to_all(lax.all_to_all(outgoing.reshape(coeffs, 3, 1, mesh_count,...  18.7 us
    all_to_all x1, waiting for transfers between devices, per_device(): lax.all_to_all(lax.all_to_all(curl_part.reshape(coeffs, 3, mesh_count, 1,...  16 us
    ppermute x2, waiting for transfers between devices, with_halo(): before = lax.ppermute(last, axis, up)  11.5 us
    unnamed x18, local copies, waits for them, and re-layouts  10.7 us
  transfers between devices with their start and end apart: 8, of which 6 were waited for; matrix products, arithmetic and copies ran while one was open for 5% of the time, Pallas kernels for 0%

commit v1 on v0

--- a/solution.py
+++ b/solution.py
@@ -75,18 +75,26 @@
     extended = jnp.concatenate([field_in, padded[:, :face_len], padded[:, 3 * face_len :]], axis=1)
     gathered = extended[:, connectivity]
     curl_part = jnp.einsum("ije,cje->cie", curl_vectors, gathered, precision=lax.Precision.HIGHEST)
-    arrived = lax.all_to_all(
+    arrived = jnp.concatenate(
         lax.all_to_all(
-            curl_part.reshape(coeffs, 3, mesh_count, 1, harm_count, 1, block_len),
-            "mesh",
-            split_axis=2,
-            concat_axis=3,
-            tiled=True,
+            jnp.stack(
+                jnp.split(
+                    lax.all_to_all(
+                        curl_part.reshape(coeffs, 3, mesh_count, 1, harm_count, 1, block_len),
+                        "mesh",
+                        split_axis=2,
+                        concat_axis=3,
+                        tiled=True,
+                    ),
+                    lax.axis_size("harm"),
+                    axis=4,
+                )
+            ),
+            "harm",
+            0,
+            0,
         ),
-        "harm",
-        split_axis=4,
-        concat_axis=5,
-        tiled=True,
+        axis=5,
     )
     arrived = arrived.reshape(coeffs, 3, mesh_count, harm_count, block_len)
     inverse, forward = dft_tables(samples)

time: 468 us -> 468 us (level)
  no operation moved by 1% of the time
where the time goes in v1:
time: 468 us; the launch traced here: 467 us
  other arithmetic  155 us (33%)
  local copies, waits for them, and re-layouts  139 us (30%)
  matrix products  79.3 us (17%)
  waiting for transfers between devices  65.2 us (14%)
  starting transfers between devices  27.6 us (6%)
    scatter-add x1, other arithmetic, per_device(): assembled = jnp.zeros((coeffs, own_edges + 2 * face_len), jnp.float32).at...  133 us
    gather x1, local copies, waits for them, and re-layouts, per_device(): gathered = extended[:, connectivity]  83.5 us
    dot_general x1, matrix products, per_device(): jnp.einsum('ije,cje->cie', curl_vectors, gathered, precision=lax.Precisio...  39.5 us
    dot_general x1, matrix products, per_device(): jnp.einsum('ije,cie->cje', curl_vectors, field_part, precision=lax.Precis...  37 us
    all_to_all x1, waiting for transfers between devices, per_device(): lax.all_to_all(lax.all_to_all(outgoing.reshape(coeffs, 3, 1, mesh_count,...  18.7 us
    all_to_all x1, waiting for transfers between devices, per_device(): lax.all_to_all(jnp.stack(jnp.split(lax.all_to_all(curl_part.reshape(coeff...  16 us
    ppermute x2, waiting for transfers between devices, with_halo(): before = lax.ppermute(last, axis, up)  11.5 us
    unnamed x18, local copies, waits for them, and re-layouts  10.7 us
  transfers between devices with their start and end apart: 8, of which 6 were waited for; matrix products, arithmetic and copies ran while one was open for 5% of the time, Pallas kernels for 0%

profile of v1, /device:TPU:1, one launch (start us, length us, event | category | flops | bytes accessed | tf_op | source)
XLA Modules:
  0.0 466.6 jit_solution(2816594935467821093)
XLA Ops:
  2.6 4.0 gather_fusion
  9.2 4.0 gather_fusion.1
  14.8 6.7 %copy.96 = f32[3,6,4096]{1,0,2:T(4,128)} copy(f32[3,6,4096]{2,1,0:T(8,128)} %param.12) | data formatting | bytes 589824 | tf_op args[3]
  22.9 3.1 pad_maximum_fusion
  25.9 83.5 %gather_fusion.2 = f32[24576,16]{1,0:T(8,128)} fusion(f32[16,7168]{0,1:T(8,128)} %pad_maximum_fusion, s32[24576]{0:T(1024)S(1)} %broadcast_clamp_fusion), kind=kCustom, calls=%fused_computation.2 | custom fusion | bytes 3244032 | tf_op jit(solution)/shard_map/gather | solution.py:76
  109.5 39.5 %fusion = f32[4096,16,3]{1,2,0:T(4,128)} fusion(f32[3,6,4096]{1,0,2:T(4,128)} %copy.96, f32[6,4096,16]{2,1,0:T(8,128)} %bitcast.94), kind=kOutput, calls=%fused_computation.6 | convolution fusion | flops 14155776 | bytes 2654208 | tf_op jit(solution)/shard_map/ije,cje->cie/dot_general | solution.py:77
  148.9 7.5 %copy.97 = f32[16,3,8,1,4,1,128]{6,0,1,4,5,3,2:T(8,128)} copy(f32[16,3,8,1,4,1,128]{0,1,6,4,2,5,3:T(4,128)} %bitcast.93) | data formatting | bytes 1572864 | tf_op jit(solution)/shard_map/reshape | solution.py:83
  156.4 3.6 all-to-all-start
  160.4 8.6 %all-to-all-done = f32[16,3,8,1,4,1,128]{6,0,1,4,5,3,2:T(8,128)S(1)} async-done(((f32[16,3,8,1,4,1,128]{6,0,1,4,5,3,2:T(8,128)}), f32[16,3,8,1,4,1,128]{6,0,1,4,5,3,2:T(8,128)S(1)}, u32[]{:S(2)}, u32[]{:S(2)}) %all-to-all-start) | async-done | bytes 786464 | tf_op jit(solution)/shard_map/all_to_all | solution.py:82
  170.1 4.8 %all-to-all-start.1 = ((f32[4,16,3,1,8,1,1,128]{7,1,4,2,6,5,3,0:T(8,128)}), f32[4,16,3,1,8,1,1,128]{7,1,4,2,6,5,3,0:T(8,128)S(1)}, u32[]{:S(2)}, u32[]{:S(2)}) async-start(f32[4,16,3,1,8,1,1,128]{7,1,4,2,6,5,3,0:T(8,128)} %copy.101), calls=%async_computation.1 | async-start | bytes 1572864 | tf_op jit(solution)/shard_map/all_to_all | solution.py:79
  177.2 16.0 %all-to-all-done.1 = f32[4,16,3,1,8,1,1,128]{7,1,4,2,6,5,3,0:T(8,128)S(1)} async-done(((f32[4,16,3,1,8,1,1,128]{7,1,4,2,6,5,3,0:T(8,128)}), f32[4,16,3,1,8,1,1,128]{7,1,4,2,6,5,3,0:T(8,128)S(1)}, u32[]{:S(2)}, u32[]{:S(2)}) %all-to-all-start.1) | async-done | bytes 786464 | tf_op jit(solution)/shard_map/all_to_all | solution.py:79
  196.9 7.7 %all-to-all-start.2 = ((f32[16,3,1,8,1,4,128]{6,0,5,1,4,2,3:T(8,128)}), f32[16,3,1,8,1,4,128]{6,0,5,1,4,2,3:T(8,128)S(1)}, u32[]{:S(2)}, u32[]{:S(2)}) async-start(f32[16,3,1,8,1,4,128]{6,0,5,1,4,2,3:T(8,128)} %copy.107), calls=%async_computation.2 | async-start | bytes 1572864 | tf_op jit(solution)/shard_map/all_to_all | solution.py:113
  204.7 9.0 %all-to-all-done.2 = f32[16,3,1,8,1,4,128]{6,0,5,1,4,2,3:T(8,128)S(1)} async-done(((f32[16,3,1,8,1,4,128]{6,0,5,1,4,2,3:T(8,128)}), f32[16,3,1,8,1,4,128]{6,0,5,1,4,2,3:T(8,128)S(1)}, u32[]{:S(2)}, u32[]{:S(2)}) %all-to-all-start.2) | async-done | bytes 786464 | tf_op jit(solution)/shard_map/all_to_all | solution.py:113
  214.7 3.5 all-to-all-start.3
  218.3 18.7 %all-to-all-done.3 = f32[16,3,8,1,1,4,128]{6,0,2,1,4,3,5:T(8,128)S(1)} async-done(((f32[16,3,8,1,1,4,128]{6,0,2,1,4,3,5:T(8,128)}), f32[16,3,8,1,1,4,128]{6,0,2,1,4,3,5:T(8,128)S(1)}, u32[]{:S(2)}, u32[]{:S(2)}) %all-to-all-start.3) | async-done | bytes 786464 | tf_op jit(solution)/shard_map/all_to_all | solution.py:112
  237.0 5.8 %copy.120 = f32[16,3,8,1,1,4,128]{0,1,6,5,2,4,3:T(4,128)} copy(f32[16,3,8,1,1,4,128]{6,0,2,1,4,3,5:T(8,128)S(1)} %all-to-all-done.3) | data formatting | bytes 1572864 | tf_op jit(solution)/shard_map/reshape | solution.py:125
  242.8 37.0 %convolution_bitcast_fusion = f32[16,6,4096]{0,1,2:T(8,128)} fusion(f32[16,3,4096]{0,1,2:T(4,128)} %bitcast.95, f32[3,6,4096]{1,0,2:T(4,128)} %copy.96), kind=kOutput, calls=%fused_computation.9 | convolution fusion | flops 14155776 | bytes 2654208 | tf_op jit(solution)/shard_map/ije,cie->cje/dot_general | solution.py:126
  279.8 9.6 %copy.112 = f32[16,6,4096]{2,1,0:T(8,128)S(1)} copy(f32[16,6,4096]{0,1,2:T(8,128)} %convolution_bitcast_fusion) | data formatting | bytes 3145728 | tf_op jit(solution)/shard_map/ije,cie->cje/transpose | solution.py:126
  291.6 7.6 %copy.113 = f32[24576,16]{1,0:T(8,128)} copy(f32[24576,16]{0,1:T(8,128)} %bitcast.97) | data formatting | bytes 3145728 | tf_op jit(solution)/shard_map/reshape | solution.py:130
  299.2 132.9 %scatter_custom_fusion = f32[16,7168]{0,1:T(8,128)} fusion(s32[24576]{0:T(1024)S(1)} %bitcast.102, f32[24576,16]{1,0:T(8,128)} %copy.113, f32[]{:T(128)} %constant.23.clone.1), kind=kCustom, calls=%fused_computation.16 | custom fusion | flops 393216 | bytes 459264 | tf_op jit(solution)/shard_map/scatter-add | solution.py:130
  433.5 5.3 %collective-permute-start.2 = (f32[16,1024]{0,1:T(8,128)S(1)}, f32[16,1024]{0,1:T(8,128)}, u32[]{:S(2)}, u32[]{:S(2)}) collective-permute-start(f32[16,1024]{0,1:T(8,128)S(1)} %get-tuple-element.8), channel_id=1, source_target_pairs={{0,4},{4,8},{8,12},{12,16},{16,20},{20,24},{24,28},{28,0},{1,5},{5... | collective-permute-start | bytes 196616 | tf_op jit(solution)/shard_map/ppermute | solution.py:17
  438.9 11.5 %collective-permute-done.2 = f32[16,1024]{0,1:T(8,128)} collective-permute-done((f32[16,1024]{0,1:T(8,128)S(1)}, f32[16,1024]{0,1:T(8,128)}, u32[]{:S(2)}, u32[]{:S(2)}) %collective-permute-start.2) | collective-permute-done | bytes 65568 | tf_op jit(solution)/shard_map/ppermute | solution.py:17
  450.4 7.4 %scatter_custom_fusion.1 = f32[16,5120]{0,1:T(8,128)S(1)} fusion(f32[16,5120]{0,1:T(8,128)S(1)} %slice-done, s32[1024]{0:T(1024)S(1)} %bitcast.106, f32[16,1024]{0,1:T(8,128)} %collective-permute-done.2), kind=kCustom, calls=%fused_computation.34 | custom fusion | flops 16384 | bytes 393216 | tf_op jit(solution)/shard_map/scatter-add | solution.py:133
  457.8 7.4 %scatter_custom_fusion.2 = f32[16,5120]{0,1:T(8,128)S(1)} fusion(f32[16,5120]{0,1:T(8,128)S(1)} %scatter_custom_fusion.1, s32[1024]{0:T(1024)S(1)} %bitcast.104, f32[16,1024]{0,1:T(8,128)} %collective-permute-done.3), kind=kCustom, calls=%fused_computation.32 | custom fusion | flops 16384 | bytes 393216 | tf_op jit(solution)/shard_map/scatter-add | solution.py:134
  (54 shorter events, 21.5 us)
Async XLA Ops:
  0.0 160.0 %copy-start = (f32[4,8]{1,0:T(4,128)S(1)}, f32[4,8]{1,0:T(4,128)}, u32[]{:S(2)}) copy-start(f32[4,8]{1,0:T(4,128)} %param.17) | copy-start | bytes 388
  0.0 13.2 %copy-start.3 = (s32[6,4096]{1,0:T(8,128)S(1)}, s32[6,4096]{1,0:T(8,128)}, u32[]{:S(2)}) copy-start(s32[6,4096]{1,0:T(8,128)} %param.11) | copy-start | bytes 294916
  6.6 14.9 %collective-permute-start = (f32[16,1024]{0,1:T(8,128)}, f32[16,1024]{0,1:T(8,128)S(1)}, u32[]{:S(2)}, u32[]{:S(2)}) collective-permute-start(f32[16,1024]{0,1:T(8,128)} %bitcast.107), channel_id=1, source_target_pairs={{0,4},{4,8},{8,12},{12,16},{16,20},{20,24},{24,28},{28,0},{1,5},{5... | collective-permute-start | bytes 196616 | tf_op jit(solution)/shard_map/ppermute | solution.py:17
  13.2 9.7 %collective-permute-start.1 = (f32[16,1024]{0,1:T(8,128)}, f32[16,1024]{0,1:T(8,128)}, u32[]{:S(2)}, u32[]{:S(2)}) collective-permute-start(f32[16,1024]{0,1:T(8,128)} %bitcast.108), channel_id=1, source_target_pairs={{4,0},{8,4},{12,8},{16,12},{20,16},{24,20},{28,24},{0,28},{5,1},{9... | collective-permute-start | bytes 196616 | tf_op jit(solution)/shard_map/ppermute | solution.py:18
  148.9 11.1 %copy-start.4 = (s32[8,128]{1,0:T(8,128)S(1)}, s32[8,128]{1,0:T(8,128)}, u32[]{:S(2)}) copy-start(s32[8,128]{1,0:T(8,128)} %param.14) | copy-start | bytes 12292
  148.9 11.4 %copy-start.5 = (s32[8]{0:T(128)S(1)}, s32[8]{0:T(128)}, u32[]{:S(2)}) copy-start(s32[8]{0:T(128)} %param.15) | copy-start | bytes 100
  148.9 11.4 %copy-start.6 = (f32[4]{0:T(128)S(1)}, f32[4]{0:T(128)}, u32[]{:S(2)}) copy-start(f32[4]{0:T(128)} %param.16) | copy-start | bytes 52
  156.4 18.6 %copy-start.2 = (f32[64,3,8,128]{3,2,1,0:T(8,128)S(1)}, f32[64,3,8,128]{3,2,1,0:T(8,128)}, u32[]{:S(2)}) copy-start(f32[64,3,8,128]{3,2,1,0:T(8,128)} %param.13) | copy-start | bytes 2359300
  156.4 12.6 %all-to-all-start = ((f32[16,3,8,1,4,1,128]{6,0,1,4,5,3,2:T(8,128)}), f32[16,3,8,1,4,1,128]{6,0,1,4,5,3,2:T(8,128)S(1)}, u32[]{:S(2)}, u32[]{:S(2)}) async-start(f32[16,3,8,1,4,1,128]{6,0,1,4,5,3,2:T(8,128)} %copy.97), calls=%async_computation | async-start | bytes 1572864 | tf_op jit(solution)/shard_map/all_to_all | solution.py:82
  170.1 23.0 %all-to-all-start.1 = ((f32[4,16,3,1,8,1,1,128]{7,1,4,2,6,5,3,0:T(8,128)}), f32[4,16,3,1,8,1,1,128]{7,1,4,2,6,5,3,0:T(8,128)S(1)}, u32[]{:S(2)}, u32[]{:S(2)}) async-start(f32[4,16,3,1,8,1,1,128]{7,1,4,2,6,5,3,0:T(8,128)} %copy.101), calls=%async_computation.1 | async-start | bytes 1572864 | tf_op jit(solution)/shard_map/all_to_all | solution.py:79
  196.9 16.9 %all-to-all-start.2 = ((f32[16,3,1,8,1,4,128]{6,0,5,1,4,2,3:T(8,128)}), f32[16,3,1,8,1,4,128]{6,0,5,1,4,2,3:T(8,128)S(1)}, u32[]{:S(2)}, u32[]{:S(2)}) async-start(f32[16,3,1,8,1,4,128]{6,0,5,1,4,2,3:T(8,128)} %copy.107), calls=%async_computation.2 | async-start | bytes 1572864 | tf_op jit(solution)/shard_map/all_to_all | solution.py:113
  214.7 22.3 %all-to-all-start.3 = ((f32[16,3,8,1,1,4,128]{6,0,2,1,4,3,5:T(8,128)}), f32[16,3,8,1,1,4,128]{6,0,2,1,4,3,5:T(8,128)S(1)}, u32[]{:S(2)}, u32[]{:S(2)}) async-start(f32[16,3,8,1,1,4,128]{6,0,2,1,4,3,5:T(8,128)} %copy.108), calls=%async_computation.3 | async-start | bytes 1572864 | tf_op jit(solution)/shard_map/all_to_all | solution.py:112
  432.1 18.2 %slice-start = ((f32[16,7168]{0,1:T(8,128)}), f32[16,5120]{0,1:T(8,128)S(1)}, s32[]{:S(2)}) async-start(f32[16,7168]{0,1:T(8,128)} %scatter_custom_fusion), calls=%async_computation.4 | async-start | bytes 5242880 | tf_op jit(solution)/shard_map/slice | solution.py:133
  433.5 16.8 %collective-permute-start.2 = (f32[16,1024]{0,1:T(8,128)S(1)}, f32[16,1024]{0,1:T(8,128)}, u32[]{:S(2)}, u32[]{:S(2)}) collective-permute-start(f32[16,1024]{0,1:T(8,128)S(1)} %get-tuple-element.8), channel_id=1, source_target_pairs={{0,4},{4,8},{8,12},{12,16},{16,20},{20,24},{24,28},{28,0},{1,5},{5... | collective-permute-start | bytes 196616 | tf_op jit(solution)/shard_map/ppermute | solution.py:17
  438.9 18.9 %collective-permute-start.3 = (f32[16,1024]{0,1:T(8,128)S(1)}, f32[16,1024]{0,1:T(8,128)}, u32[]{:S(2)}, u32[]{:S(2)}) collective-permute-start(f32[16,1024]{0,1:T(8,128)S(1)} %get-tuple-element.7), channel_id=1, source_target_pairs={{4,0},{8,4},{12,8},{16,12},{20,16},{24,20},{28,24},{0,28},{5,1},{9... | collective-permute-start | bytes 196616 | tf_op jit(solution)/shard_map/ppermute | solution.py:18
  450.4 16.3 %copy-start.1 = (f32[4,8]{1,0:T(4,128)S(1)}, f32[4,8]{1,0:T(4,128)}, u32[]{:S(2)}) copy-start(f32[4,8]{1,0:T(4,128)} %param.17) | copy-start | bytes 388
